TPU v7x, 256 devices: a 8x8x2 block of a 8x8x16 slice. The times are simulated.
256 devices in a mesh: groups: 2 (over z), ep: 16 (over x, core), tp: 8 (over y).
Axes of the slice: x: 8, y: 8, z: 2, core: 2. Of those that a mesh axis runs over, the one named last changes fastest.
The devices are a block of a 8x8x16 slice.
Arguments:
- tokens: bfloat16 [1024, 7168], P(('groups', 'ep')), parts along dimension 0, may hold values from -6 to 6
- w_gate: bfloat16 [16, 7168, 2048], P('ep', None, 'tp'), may hold values from -0.0625 to 0.0625
- w_up: bfloat16 [16, 7168, 2048], P('ep', None, 'tp'), may hold values from -0.0625 to 0.0625
- w_down: bfloat16 [16, 2048, 7168], P('ep', 'tp'), may hold values from -0.1875 to 0.1875
- router_logits: float32 [1024, 8], P(('groups', 'ep')), parts along dimension 0, may hold values from -6 to 6
- expert_ids: int32 [1024, 8], P(('groups', 'ep')), parts along dimension 0, may hold values from 0 to 15, all different within a row; in each aligned block of 32 rows (0 to 31, 32 to 63, ...) at most 24 rows name the same one
- draft_lengths: int32 [128], P(('groups', 'ep')), parts along dimension 0, may hold values from 7 to 8
- accept_mask: int32 [128, 8], P(('groups', 'ep')), parts along dimension 0, may hold values 0 or 1
Outputs:
- mixed: bfloat16 [1024, 7168], P(('groups', 'ep'), 'tp'), parts along dimension 0
- accepted: int32 [2], P('groups'), parts along dimension 0
There are 2 independent parts, one for each index of `groups`. A program takes and returns all parts, laid end to end along the dimension named above; an argument that names none is the same for every part. Nothing has to cross between parts.
Inputs may be any that keep to these rules, and one draw needn't show every extreme that they name: `expert_ids`: each row names 8 different experts. Among the rows of one ep index (aligned blocks of 32 rows) no expert is named by more than 24 rows, and in every draw some expert is named by exactly 24 rows of some block.
All inputs are finite; a program needn't handle non-finite values. No bound on the sum of `accept_mask` on one device may be relied on, other than what follows from the above.
Results may differ from a plain program's by a relative error of at most 0.017.
Values may be sent and summed in bfloat16 or wider, within the bound.
No kernel may reach another device: no remote copies, remote signals or barrier semaphores. Data moves between devices by JAX's collectives and lax.ppermute only.
A program may use at most 128 MiB of HBM per device.

v0:
```python
import jax
import jax.numpy as jnp
from jax import lax
from jax.sharding import PartitionSpec as P

DRAFT = 8
EXPERTS = 16
CAP = 24


def sent_to_all(array, axis):
    copies = jnp.broadcast_to(array, (lax.axis_size(axis), *array.shape))
    return lax.all_to_all(copies, axis, split_axis=0, concat_axis=0, tiled=True)


def of_everyone(array, axis):
    everything = sent_to_all(array, axis)
    return jnp.sum(everything, axis=0)


def per_device(tokens, w_gate, w_up, w_down, router_logits, expert_ids, draft_lengths, accept_mask):
    tok_rows = tokens.shape[0]
    width = tokens.shape[1]
    top = expert_ids.shape[1]
    tp_count = lax.axis_size("tp")
    slice_width = width // tp_count
    live = jnp.arange(DRAFT, dtype=jnp.int32)[None, :] < draft_lengths[:, None]
    live_rows = live.reshape(tok_rows)
    live_tokens = jnp.where(live_rows[:, None], tokens, jnp.zeros((), tokens.dtype))
    sig = jax.nn.sigmoid(router_logits)
    gates = 2.827 * sig / jnp.sum(sig, axis=1, keepdims=True)
    flat_ids = expert_ids.reshape(-1)
    onehot = (flat_ids[:, None] == jnp.arange(EXPERTS, dtype=jnp.int32)[None, :]).astype(jnp.int32)
    rank = jnp.cumsum(onehot, axis=0) - 1
    slot = jnp.sum(rank * onehot, axis=1)
    target = flat_ids * CAP + slot
    source = jnp.arange(tok_rows * top, dtype=jnp.int32) // top
    own_cols = lax.dynamic_slice_in_dim(
        live_tokens, lax.axis_index("tp") * slice_width, slice_width, 1
    )
    sendbuf = jnp.zeros((EXPERTS * CAP, slice_width), tokens.dtype).at[target].set(own_cols[source])
    received = lax.all_to_all(
        sendbuf.reshape(EXPERTS, CAP, slice_width), "ep", split_axis=0, concat_axis=1, tiled=True
    )
    piece = lax.all_gather(received, "tp", axis=2, tiled=True)
    gate_sum = jnp.einsum("emd,edf->emf", piece, w_gate, preferred_element_type=jnp.float32)
    up_sum = jnp.einsum("emd,edf->emf", piece, w_up, preferred_element_type=jnp.float32)
    hidden = (jax.nn.silu(gate_sum) * up_sum).astype(jnp.bfloat16)
    partial_value = jnp.einsum("emf,efd->emd", hidden, w_down, preferred_element_type=jnp.float32)
    expert_out = lax.psum_scatter(
        partial_value.astype(jnp.bfloat16), "tp", scatter_dimension=2, tiled=True
    )
    returned = lax.all_to_all(expert_out, "ep", split_axis=1, concat_axis=0, tiled=True)
    flat_back = returned.reshape(EXPERTS * CAP, returned.shape[2])
    picked = flat_back[target].reshape(tok_rows, top, returned.shape[2])
    mixed = jnp.sum(gates[:, :, None] * picked.astype(jnp.float32), axis=1).astype(jnp.bfloat16)
    passed = accept_mask * live.astype(jnp.int32)
    prefix = jnp.cumprod(passed, axis=1)
    local_count = jnp.sum(prefix)
    total = of_everyone(local_count, "ep")
    accepted = total.reshape(1)
    return (mixed, accepted)


def solution(mesh):
    placed = (
        P(("groups", "ep"), None),
        P("ep", None, "tp"),
        P("ep", None, "tp"),
        P("ep", "tp", None),
        P(("groups", "ep"), None),
        P(("groups", "ep"), None),
        P(("groups", "ep")),
        P(("groups", "ep"), None),
    )
    return jax.shard_map(
        per_device,
        mesh=mesh,
        in_specs=placed,
        out_specs=(P(("groups", "ep"), "tp"), P("groups")),
        check_vma=False,
    )
```

profile of v0, /device:TPU:513, one launch (start us, length us, event | category | flops | bytes accessed | tf_op | source)
XLA Modules:
  0.0 286.3 jit_solution(15594155464627464665)
XLA Ops:
  7.2 0.1 all-gather.2.cloned.1.call-start
  7.2 0.8 copy.36
  8.0 0.1 eq.29
  8.1 0.1 eq.25
  8.2 0.7 broadcast_multiply_fusion
  8.9 0.6 reduce-window.6
  9.5 0.2 slice_reduce_fusion
  9.7 0.1 copy.35
  9.8 0.1 mul.55
  9.9 0.7 iota_compare_fusion.2
  10.6 0.1 lt.48
  10.7 0.1 fusion.23
  10.8 0.9 dynamic-slice_select_fusion
  11.7 3.5 %scatter_custom_fusion = bf16[384,896]{1,0:T(8,128)(2,1)S(1)} fusion(s32[256]{0:T(256)S(1)} %bitcast.67, bf16[32,896]{1,0:T(8,128)(2,1)S(1)} %dynamic-slice_select_fusion, s32[1024]{0:T(1024)S(1)} %pad_clamp_fusion.1, bf16[]{:T(256)} %constant.43.clone.1), kind=kCustom, calls=%fused_computation.19 | custom fusion | bytes 688130 | tf_op jit(solution)/shard_map/scatter | solution.py:41
  15.2 44.7 %all_to_all.27 = bf16[16,24,896]{2,1,0:T(8,128)(2,1)} all-to-all(bf16[16,24,896]{2,1,0:T(8,128)(2,1)S(1)} %bitcast.66), channel_id=1, replica_groups=mesh['groups'=2,'ep'=16,'tp'=8] {'ep'}, dimensions={0} | all-to-all | bytes 1376256 | tf_op jit(solution)/shard_map/all_to_all | solution.py:42
  59.9 0.1 all-gather.2.cloned.1.call-update
  60.0 0.1 reduce-scatter.4.cloned.1.call-start
  60.1 66.0 %all-gather.2.cloned.1.call-done = bf16[1,384,7168]{2,1,0:T(8,128)(2,1)} async-done(((bf16[1,384,896]{2,1,0:T(8,128)(2,1)}), bf16[1,384,7168]{2,1,0:T(8,128)(2,1)}) %all-gather.2.cloned.1.call-update) | async-done | bytes 5505040 | tf_op jit(solution)/shard_map/all_gather | solution.py:45
  126.1 5.4 %fusion.3 = f32[384,256]{1,0:T(8,128)S(1)} fusion(bf16[1,384,7168]{2,1,0:T(8,128)(2,1)} %all-gather.2.cloned.1.call-done, bf16[1,7168,256]{2,1,0:T(8,128)(2,1)} %param.9), kind=kOutput, calls=%fused_computation.8 | convolution fusion | flops 1409286144 | bytes 9568256 | tf_op jit(solution)/shard_map/emd,edf->emf/dot_general | solution.py:46
  131.5 0.9 copy-done.5
  132.4 1.6 fusion.13
  134.0 0.4 copy-done
  134.4 4.0 %fusion = bf16[1,384,7168]{2,1,0:T(8,128)(2,1)} fusion(bf16[384,256]{1,0:T(8,128)(2,1)S(1)} %fusion.13, bf16[1,256,7168]{2,1,0:T(8,128)(2,1)S(1)} %copy-done), kind=kOutput, calls=%fused_computation.4 | convolution fusion | flops 1412038656 | bytes 9371648 | tf_op jit(solution)/shard_map/emf,efd->emd/dot_general | solution.py:49
  138.4 24.0 %copy.41 = bf16[1,384,7168]{1,0,2:T(2,128)(2,1)} copy(bf16[1,384,7168]{2,1,0:T(8,128)(2,1)} %fusion) | data formatting | bytes 11010048
  162.4 7.4 %copy.51 = bf16[7168,1,384]{2,0,1:T(8,128)(2,1)} copy(bf16[7168,1,384]{2,1,0:T(2,128)(2,1)} %bitcast.60) | data formatting | bytes 11010048
  169.8 0.1 reduce-scatter.4.cloned.1.call-update
  169.9 0.6 copy-done.2
  170.5 0.1 broadcast_select_fusion
  170.6 0.2 reduce_window.9
  170.8 0.6 reduce_sum.51
  171.4 1.2 broadcast_in_dim.29
  172.6 7.6 %all-to-all-start.2 = ((s32[16,1,1]{2,1,0:T(1,128)}), s32[16,1,1]{2,1,0:T(1,128)S(1)}, u32[]{:S(2)}, u32[]{:S(2)}) async-start(s32[16,1,1]{2,1,0:T(1,128)} %broadcast_in_dim.29), calls=%async_computation.2 | async-start | bytes 16384 | tf_op jit(solution)/shard_map/all_to_all | solution.py:13
  180.2 57.8 %reduce-scatter.4.cloned.1.call-done = bf16[896,384]{1,0:T(8,128)(2,1)} async-done(((bf16[7168,384]{1,0:T(8,128)(2,1)}), bf16[896,384]{1,0:T(8,128)(2,1)}) %reduce-scatter.4.cloned.1.call-update) | async-done | bytes 688144
  238.0 1.8 reshape_bitcast_fusion
  239.8 0.0 copy-start.1
  239.8 2.3 copy.39
  242.1 0.5 broadcast.160
  242.6 4.8 %reduce.3 = bf16[384,896]{1,0:T(8,128)(2,1)S(1)} reduce(bf16[384,1,896]{2,1,0:T(2,128)(2,1)S(1)} %bitcast.63, bf16[]{:T(256)} %broadcast.160), dimensions={1}, to_apply=%bitcast.54.reduce_sub_computation | reduce | bytes 1376258
  247.5 1.0 reshape.202
  248.5 0.0 all-to-all-done.2
  248.5 7.4 %all-to-all-start.1 = ((bf16[16,2,10752]{2,1,0:T(2,128)(2,1)}), bf16[16,2,10752]{2,1,0:T(2,128)(2,1)S(1)}, u32[]{:S(2)}, u32[]{:S(2)}) async-start(bf16[16,2,10752]{2,1,0:T(2,128)(2,1)} %reshape.202), calls=%async_computation.1 | async-start | bytes 1376256 | tf_op jit(solution)/shard_map/all_to_all | solution.py:53
  256.0 0.1 copy.34
  256.1 0.7 reduce_sum.52
  256.7 19.8 %all-to-all-done.1 = bf16[16,2,10752]{2,1,0:T(2,128)(2,1)S(1)} async-done(((bf16[16,2,10752]{2,1,0:T(2,128)(2,1)}), bf16[16,2,10752]{2,1,0:T(2,128)(2,1)S(1)}, u32[]{:S(2)}, u32[]{:S(2)}) %all-to-all-start.1) | async-done | bytes 688160 | tf_op jit(solution)/shard_map/all_to_all | solution.py:53
  276.6 0.6 reshape.203
  277.2 0.1 copy.52
  277.2 1.2 gather_fusion
  278.4 1.0 fusion.18
  (17 shorter events, 0.1 us)
Async XLA Ops:
  7.2 118.9 %all-gather.2.cloned.1.call-start = ((), (), s32[]{:S(2)}) async-start(), calls=%async_computation.4 | async-start | bytes 6193152 | tf_op jit(solution)/shard_map/all_gather | solution.py:45
  60.0 178.0 %reduce-scatter.4.cloned.1.call-start = ((), (), s32[]{:S(2)}) async-start(), calls=%async_computation.5 | async-start | bytes 6193152
  126.1 5.4 %copy-start.4 = (bf16[1,384,7168]{2,1,0:T(8,128)(2,1)S(1)}, bf16[1,384,7168]{2,1,0:T(8,128)(2,1)}, u32[]{:S(2)}) copy-start(bf16[1,384,7168]{2,1,0:T(8,128)(2,1)} %all-gather.2.cloned.1.call-done) | copy-start | bytes 16515076
  126.1 6.3 %copy-start.5 = (bf16[1,7168,256]{2,1,0:T(8,128)(2,1)S(1)}, bf16[1,7168,256]{2,1,0:T(8,128)(2,1)}, u32[]{:S(2)}) copy-start(bf16[1,7168,256]{2,1,0:T(8,128)(2,1)} %param.10) | copy-start | bytes 11010052
  132.4 2.0 copy-start
  169.8 0.7 copy-start.2
  169.8 0.7 copy-start.3
  172.6 75.9 %all-to-all-start.2 = ((s32[16,1,1]{2,1,0:T(1,128)}), s32[16,1,1]{2,1,0:T(1,128)S(1)}, u32[]{:S(2)}, u32[]{:S(2)}) async-start(s32[16,1,1]{2,1,0:T(1,128)} %broadcast_in_dim.29), calls=%async_computation.2 | async-start | bytes 16384 | tf_op jit(solution)/shard_map/all_to_all | solution.py:13
  239.8 16.2 %copy-start.1 = (f32[32,8]{0,1:T(8,128)S(1)}, f32[32,8]{0,1:T(8,128)}, u32[]{:S(2)}) copy-start(f32[32,8]{0,1:T(8,128)} %param.12) | copy-start | bytes 3076
  248.5 28.1 %all-to-all-start.1 = ((bf16[16,2,10752]{2,1,0:T(2,128)(2,1)}), bf16[16,2,10752]{2,1,0:T(2,128)(2,1)S(1)}, u32[]{:S(2)}, u32[]{:S(2)}) async-start(bf16[16,2,10752]{2,1,0:T(2,128)(2,1)} %reshape.202), calls=%async_computation.1 | async-start | bytes 1376256 | tf_op jit(solution)/shard_map/all_to_all | solution.py:53
Sparse Core Ops, SparseCore 0:
  60.1 65.8 all-gather.1
  170.0 67.9 reduce-scatter.3
where the time goes:
time: 288 us; the launch traced here: 286 us
  waiting for transfers between devices  144 us (50%)
  local copies, waits for them, and re-layouts  47.2 us (16%)
  blocking collectives  44.7 us (16%)
  starting transfers between devices  15.1 us (5%)
  between operations  14.2 us (5%)
  matrix products  10.9 us (4%)
  other arithmetic  10.4 us (4%)
    all_gather x1, waiting for transfers between devices, per_device(): piece = lax.all_gather(received, 'tp', axis=2, tiled=True)  66 us
    unnamed x3, waiting for transfers between devices  57.9 us
    all_to_all x1, blocking collectives, per_device(): lax.all_to_all(sendbuf.reshape(EXPERTS, CAP, slice_width), 'ep', split_ax...  44.7 us
    unnamed x20, local copies, waits for them, and re-layouts  38.2 us
    all_to_all x1, waiting for transfers between devices, per_device(): lax.all_to_all(expert_out, 'ep', split_axis=1, concat_axis=0, tiled=True)  19.8 us
    all_to_all x1, starting transfers between devices, sent_to_all(): return lax.all_to_all(copies, axis, split_axis=0, concat_axis=0, tiled=True)  7.55 us
    all_to_all x1, starting transfers between devices, per_device(): lax.all_to_all(expert_out, 'ep', split_axis=1, concat_axis=0, tiled=True)  7.44 us
  transfers between devices with their start and end apart: 4, of which 3 were waited for; matrix products, arithmetic and copies ran while one was open for 5% of the time, Pallas kernels for 0%

commit v1 on v0

v1 whole, which is shorter than its diff:
```python
import functools
import jax
import jax.numpy as jnp
from jax import lax
from jax.experimental import pallas as pl
from jax.experimental.pallas import tpu as pltpu
from jax.sharding import PartitionSpec as P

DRAFT = 8


def ffn_kernel(n, x_ref, wg_ref, wu_ref, wd_ref, gate_ref, o_ref, acc_g, acc_u, hid):
    step = pl.program_id(0)

    @pl.when(step == 0)
    def _():
        acc_g[...] = jnp.zeros_like(acc_g)
        acc_u[...] = jnp.zeros_like(acc_u)

    @pl.when(step < n)
    def _():
        x = x_ref[...].reshape(acc_g.shape[0], x_ref.shape[3])
        acc_g[...] += jnp.dot(x, wg_ref[0], preferred_element_type=jnp.float32)
        acc_u[...] += jnp.dot(x, wu_ref[0], preferred_element_type=jnp.float32)

    @pl.when(step == n - 1)
    def _():
        g = acc_g[...]
        hid[...] = (g / (1.0 + jnp.exp(-g)) * acc_u[...]).astype(jnp.bfloat16)

    @pl.when(step >= n)
    def _():
        p = jnp.dot(hid[...], wd_ref[0], preferred_element_type=jnp.float32)
        p = p * gate_ref[...]
        o_ref[...] = p.astype(jnp.bfloat16).reshape(o_ref.shape)


def expert(gathered, w_gate, w_up, w_down, gate):
    ep, n, rows, width = gathered.shape
    units = w_gate.shape[2]
    total = ep * rows
    return pl.pallas_call(
        functools.partial(ffn_kernel, n),
        grid=(2 * n,),
        in_specs=[
            pl.BlockSpec((ep, 1, rows, width), lambda s: (0, jnp.minimum(s, n - 1), 0, 0)),
            pl.BlockSpec((1, width, units), lambda s: (0, jnp.minimum(s, n - 1), 0)),
            pl.BlockSpec((1, width, units), lambda s: (0, jnp.minimum(s, n - 1), 0)),
            pl.BlockSpec((1, units, width), lambda s: (0, 0, jnp.maximum(s - n, 0))),
            pl.BlockSpec((total, 1), lambda s: (0, 0)),
        ],
        out_specs=pl.BlockSpec((ep, 1, rows, width), lambda s: (0, jnp.maximum(s - n, 0), 0, 0)),
        out_shape=jax.ShapeDtypeStruct(gathered.shape, jnp.bfloat16),
        scratch_shapes=[
            pltpu.VMEM((total, units), jnp.float32),
            pltpu.VMEM((total, units), jnp.float32),
            pltpu.VMEM((total, units), jnp.bfloat16),
        ],
        cost_estimate=pl.CostEstimate(
            flops=6 * total * n * width * units,
            bytes_accessed=4 * total * n * width + 6 * n * width * units,
            transcendentals=total * units,
        ),
        compiler_params=pltpu.CompilerParams(dimension_semantics=("arbitrary",)),
    )(gathered, w_gate, w_up, w_down, gate)


def per_device(tokens, w_gate, w_up, w_down, router_logits, expert_ids, draft_lengths, accept_mask):
    rows, width = tokens.shape
    ep = lax.axis_size("ep")
    tp = lax.axis_size("tp")
    slice_width = width // tp
    live = jnp.arange(DRAFT, dtype=jnp.int32)[None, :] < draft_lengths[:, None]
    live_rows = live.reshape(rows)
    own_cols = lax.dynamic_slice_in_dim(tokens, lax.axis_index("tp") * slice_width, slice_width, 1)
    own_cols = jnp.where(live_rows[:, None], own_cols, jnp.zeros((), tokens.dtype))
    gathered = lax.all_gather(own_cols, ("ep", "tp"), axis=0)
    gathered = gathered.reshape(ep, tp, rows, slice_width)

    sig = jax.nn.sigmoid(router_logits)
    gates = 2.827 * sig / jnp.sum(sig, axis=1, keepdims=True)
    named = expert_ids[:, None, :] == jnp.arange(ep, dtype=jnp.int32)[None, :, None]
    dense = jnp.sum(jnp.where(named, gates[:, None, :], 0.0), axis=2)
    dense = jnp.where(live_rows[:, None], dense, 0.0)
    passed = accept_mask * live.astype(jnp.int32)
    count = jnp.sum(jnp.cumprod(passed, axis=1)).astype(jnp.float32)
    sent = jnp.concatenate([dense.T, jnp.broadcast_to(count, (ep, 1))], axis=1)
    got = lax.all_to_all(sent, "ep", split_axis=0, concat_axis=0, tiled=True)
    accepted = jnp.sum(got[:, rows]).astype(jnp.int32).reshape(1)
    gate = got[:, :rows].reshape(ep * rows, 1)

    out = expert(gathered, w_gate, w_up, w_down, gate)
    mixed = lax.psum_scatter(out.reshape(ep * tp, rows, slice_width), ("ep", "tp"), scatter_dimension=0)
    return mixed, accepted


def solution(mesh):
    placed = (
        P(("groups", "ep"), None),
        P("ep", None, "tp"),
        P("ep", None, "tp"),
        P("ep", "tp", None),
        P(("groups", "ep"), None),
        P(("groups", "ep"), None),
        P(("groups", "ep")),
        P(("groups", "ep"), None),
    )
    return jax.shard_map(
        per_device,
        mesh=mesh,
        in_specs=placed,
        out_specs=(P(("groups", "ep"), "tp"), P("groups")),
        check_vma=False,
    )
```

time: 288 us -> 338 us (1.17)
  waiting for transfers between devices: 144 us -> 261 us
  local copies, waits for them, and re-layouts: 47.2 us -> 1.06 us
  Pallas kernels: 0 us -> 18.4 us
  starting transfers between devices: 15.1 us -> 0.13 us
  blocking collectives: 44.7 us -> 30 us
  matrix products: 10.9 us -> 0 us
  other arithmetic: 10.4 us -> 6.71 us
    reduce_scatter x0 -> x1, waiting for transfers between devices: none -> 192 us  [per_device(): lax.psum_scatter(out.reshape(ep * tp, rows, slice_width), ('ep', 'tp'), s...]
    unnamed x3 -> x2, waiting for transfers between devices: 57.9 us -> 0.11 us
    unnamed x20 -> x0, local copies, waits for them, and re-layouts: 38.2 us -> none
    all_to_all x2 -> x0, waiting for transfers between devices: 19.8 us -> none  [the longest x1 19.8 us: per_device(): lax.all_to_all(expert_out, 'ep', split_axis=1, concat_axis=0, tiled=True)]
    pallas_call x0 -> x1, Pallas kernels: none -> 18.4 us  [expert(): pl.pallas_call(functools.partial(ffn_kernel, n), grid=(2 * n,), in_specs=...]
    all_to_all x2 -> x0, starting transfers between devices: 15 us -> none  [the longest x1 7.55 us: sent_to_all(): return lax.all_to_all(copies, axis, split_axis=0, concat_axis=0, tiled=True)]
    all_to_all x1, blocking collectives: 44.7 us -> 30 us  [per_device(): got = lax.all_to_all(sent, 'ep', split_axis=0, concat_axis=0, tiled=True)]
    dot_general x3 -> x0, matrix products: 10.9 us -> none  [the longest x1 5.39 us: per_device(): jnp.einsum('emd,edf->emf', piece, w_gate, preferred_element_type=jnp.floa...]
  transfers between devices with their start and end apart: 4 -> 2, of which waited for: 3 -> 2; matrix products, arithmetic and copies ran while one was open for 5% -> 2% of each run, Pallas kernels for 0% -> 0%
where the time goes in v1:
time: 338 us; the launch traced here: 334 us
  waiting for transfers between devices  261 us (77%)
  blocking collectives  30 us (9%)
  Pallas kernels  18.4 us (5%)
  between operations  16.6 us (5%)
  other arithmetic  6.71 us (2%)
    reduce_scatter x1, waiting for transfers between devices, per_device(): lax.psum_scatter(out.reshape(ep * tp, rows, slice_width), ('ep', 'tp'), s...  192 us
    all_gather x1, waiting for transfers between devices, per_device(): gathered = lax.all_gather(own_cols, ('ep', 'tp'), axis=0)  68.8 us
    all_to_all x1, blocking collectives, per_device(): got = lax.all_to_all(sent, 'ep', split_axis=0, concat_axis=0, tiled=True)  30 us
    pallas_call x1, Pallas kernels, expert(): pl.pallas_call(functools.partial(ffn_kernel, n), grid=(2 * n,), in_specs=...  18.4 us
  transfers between devices with their start and end apart: 2, of which 2 were waited for; matrix products, arithmetic and copies ran while one was open for 2% of the time, Pallas kernels for 0%

profile of v1, /device:TPU:513, one launch (start us, length us, event | category | flops | bytes accessed | tf_op | source)
XLA Modules:
  0.0 333.9 jit_solution(11020903253103597142)
XLA Ops:
  7.2 0.1 all-gather.3.cloned.1.call-start
  7.2 0.7 iota_compare_fusion.1
  8.0 0.1 lt.26
  8.1 1.5 dynamic-slice_select_fusion
  9.6 0.1 all-gather.3.cloned.1.call-update
  9.6 0.1 reduce-scatter.2.cloned.1.call-start
  9.7 0.8 broadcast_select_fusion
  10.5 0.2 reduce_window.9
  10.7 0.6 reduce_sum.38
  11.9 0.7 fusion
  12.7 0.7 multiply_divide_fusion
  13.4 0.7 select_reduce_fusion
  14.1 30.0 %all_to_all.12 = f32[16,1,33]{2,1,0:T(1,128)S(1)} all-to-all(f32[16,1,33]{2,1,0:T(1,128)S(1)} %bitcast.15), channel_id=1, replica_groups=mesh['groups'=2,'ep'=16,'tp'=8] {'ep'}, dimensions={0} | all-to-all | bytes 4224 | tf_op jit(solution)/shard_map/all_to_all | solution.py:88
  44.1 1.0 reshape.42.gate_ref
  45.1 68.8 %all-gather.3.cloned.1.call-done = bf16[4096,896]{1,0:T(8,128)(2,1)} async-done(((bf16[32,896]{1,0:T(8,128)(2,1)}), bf16[4096,896]{1,0:T(8,128)(2,1)}) %all-gather.3.cloned.1.call-update) | async-done | bytes 7340048 | tf_op jit(solution)/shard_map/all_gather | solution.py:77
  113.8 18.4 %shard_map.95 = bf16[16,8,32,896]{3,2,1,0:T(8,128)(2,1)} custom-call(bf16[16,8,32,896]{3,2,1,0:T(8,128)(2,1)} %bitcast.12, bf16[1,7168,256]{2,1,0:T(8,128)(2,1)} %wg_ref.1, bf16[1,7168,256]{2,1,0:T(8,128)(2,1)} %wu_ref.1, bf16[1,256,7168]{2,1,0:T(8,128)(2,1)} %wd_ref.1, f32[512,1]{1,0:T(8,128)} %reshape.42.gate_ref), custom_call_target="tpu_custom_call" | custom-call | flops 5637144576 | bytes 25690112 | tf_op jit(solution)/shard_map/pallas_call | solution.py:42
  132.2 0.1 reduce-scatter.2.cloned.1.call-update
  132.3 0.8 slice_reduce_fusion
  133.7 192.2 %reduce-scatter.2.cloned.1.call-done = bf16[1,32,896]{2,1,0:T(8,128)(2,1)} async-done(((bf16[128,32,896]{2,1,0:T(8,128)(2,1)}), bf16[1,32,896]{2,1,0:T(8,128)(2,1)}) %reduce-scatter.2.cloned.1.call-update) | async-done | bytes 57360 | tf_op jit(solution)/shard_map/reduce_scatter | solution.py:93
  (2 shorter events, 0.0 us)
Async XLA Ops:
  7.2 106.6 %all-gather.3.cloned.1.call-start = ((), (), s32[]{:S(2)}) async-start(), calls=%async_computation.3 | async-start | bytes 7397376 | tf_op jit(solution)/shard_map/all_gather | solution.py:77
  9.6 316.3 %reduce-scatter.2.cloned.1.call-start = ((), (), s32[]{:S(2)}) async-start(), calls=%async_computation.2 | async-start | bytes 7397376 | tf_op jit(solution)/shard_map/reduce_scatter | solution.py:93
Sparse Core Ops, SparseCore 0:
  11.2 102.5 all-gather.2
  132.4 193.4 reduce-scatter.1
